TPU v7x, 256 devices: a whole 4x4x8 slice. The times are simulated.
256 devices in a mesh: store: 16 (over x, y_hi, core), tp: 16 (over y_lo, z).
Axes of the slice: x: 4, y: 4 (y_hi: 2, y_lo: 2; y = y_hi * 2 + y_lo), z: 8, core: 2. Of those that a mesh axis runs over, the one named last changes fastest.
Arguments:
- hidden: bfloat16 [16, 576, 8192], P('store', None, 'tp'), may hold values from -300 to 300
- w_query: bfloat16 [8192, 4096], P(None, 'tp'), may hold values from -0.0625 to 0.0625
- w_keyvalue: bfloat16 [8192, 1024], P('tp'), may hold values from -0.1875 to 0.1875
- passage_cache: bfloat16 [64, 4, 384, 256], P('store'), may hold values from -400 to 400
- passage_ids: int32 [16, 8], replicated, may hold values from 0 to 63, as said below
- select_index: int32 [16, 576], P('store'), may hold values from 0 to 3071, as said below
- select_count: int32 [16], P('store'), may hold values from 288 to 576, as said below
Outputs:
- context: bfloat16 [16, 576, 4096], P('store', None, 'tp')
Inputs may be any that keep to these rules, and one draw needn't show every extreme that they name: `passage_ids`: the passages of one prompt lie in distinct shards of the pool, shard = id // 4. `select_index`: all entries of a row are distinct positions of the prompt; the first select_count[p] of row p are in increasing order, the others are ignored. `select_count`: some prompt of every draw has 576 selected tokens.
All inputs are finite; a program needn't handle non-finite values.
Results may differ from a plain program's by a relative error of at most 0.04.
Values may be sent and summed in bfloat16 or wider, within the bound.
A program may use at most 128 MiB of HBM per device.

v0:
```python
import jax
import jax.numpy as jnp
from jax import lax
from jax.sharding import Mesh
from jax.sharding import PartitionSpec as P

D = 8192
KV_HEADS = 4
HEAD_DIM = 128
PASSAGE = 384
PASSAGES = 8
SEQ = 3072
TP = ("tp_0", "tp_1")
ROPE_BASE = 1000000.0
EPSILON = 1e-06


def in_blocks(value, dim, length):
    shape = value.shape
    parts = value.reshape(*shape[:dim], length, shape[dim] // length, *shape[dim + 1 :])
    return jnp.moveaxis(parts, dim, 0)


def summed_on_arrival(value, axis, dim):
    parts = in_blocks(value, dim, lax.axis_size(axis))
    arrived = lax.all_to_all(parts, axis, split_axis=0, concat_axis=0, tiled=True)
    return arrived.astype(jnp.float32).sum(axis=0)


def from_partner(value, axis, bit):
    return lax.ppermute(value, axis, [(i, i ^ 1 << bit) for i in range(lax.axis_size(axis))])


def joined_along(parts, dim):
    shape = list(parts.shape[1:])
    shape[dim] *= parts.shape[0]
    return jnp.moveaxis(parts, 0, dim).reshape(shape)


def stacked_from(value, axes, sequence):
    parts = value[None]
    for k in sequence:
        parts = lax.all_gather(parts, axes[k], axis=0, tiled=True)
    held = [lax.axis_size(axes[k]) for k in reversed(sequence)]
    parts = parts.reshape(*held, *value.shape)
    turned = sorted(range(len(sequence)), key=lambda place: sequence[len(sequence) - 1 - place])
    return parts.transpose(*turned, *range(len(sequence), parts.ndim)).reshape(-1, *value.shape)


def gather_axes(value, axes, sequence, dim):
    return joined_along(stacked_from(value, axes, sequence), dim)


def rotate(vectors, positions):
    half_dim = vectors.shape[-1] // 2
    frequency = ROPE_BASE ** (-(jnp.arange(half_dim, dtype=jnp.float32) * 2.0) / vectors.shape[-1])
    angles = positions.astype(jnp.float32)[..., None] * frequency
    cosine = jnp.cos(angles)
    sine_part = jnp.sin(angles)
    front_half = vectors[..., :half_dim]
    back_half = vectors[..., half_dim:]
    return jnp.concatenate(
        [front_half * cosine - back_half * sine_part, back_half * cosine + front_half * sine_part],
        axis=-1,
    )


def local(hidden, w_query, w_keyvalue, passage_cache, passage_ids, select_index, select_count):
    tp_count = lax.axis_size(TP)
    group_width = tp_count // KV_HEADS
    tp_rank = lax.axis_index(TP)
    kv_head = tp_rank // group_width
    store_rank = lax.axis_index("store")
    local_heads = w_query.shape[1] // HEAD_DIM
    row_count = hidden.shape[1]
    pool_dev = passage_cache.shape[0]
    partial_kv = jnp.dot(hidden[0], w_keyvalue, preferred_element_type=jnp.float32)
    head_kv = summed_on_arrival(partial_kv.astype(jnp.bfloat16), TP, 1)
    levels = group_width.bit_length() - 1
    for level in range(levels):
        partner = from_partner(head_kv.astype(jnp.bfloat16), TP, level).astype(head_kv.dtype)
        upper = tp_rank // 2**level % 2 == 1
        head_kv = jnp.where(
            upper,
            jnp.concatenate([partner, head_kv], axis=1),
            jnp.concatenate([head_kv, partner], axis=1),
        )
    token_part = gather_axes(hidden, TP, (0, 1), 2)[0]
    widened = token_part.astype(jnp.float32)
    running = jnp.dot(token_part, w_query, preferred_element_type=jnp.float32)
    squares = jnp.sum(widened * widened, axis=-1)
    inverse_rms = lax.rsqrt(squares / D + EPSILON)
    positions = select_index[0]
    live_count = select_count[0]
    queries = rotate(
        (running * inverse_rms[:, None]).reshape(row_count, local_heads, HEAD_DIM),
        positions[:, None],
    )
    queries = (queries * HEAD_DIM ** (-0.5)).astype(jnp.bfloat16)
    key_value = head_kv * inverse_rms[:, None]
    new_keys = rotate(key_value[:, :HEAD_DIM], positions).astype(jnp.bfloat16)
    new_values = key_value[:, HEAD_DIM:].astype(jnp.bfloat16)
    head_cache = lax.dynamic_index_in_dim(passage_cache, kv_head, 1, keepdims=False)
    owners = passage_ids // pool_dev
    local_index = passage_ids % pool_dev
    matches = owners == store_rank
    local_slot = jnp.sum(jnp.where(matches, local_index, 0), axis=1)
    present = jnp.any(matches, axis=1)
    outgoing = jnp.take(head_cache, local_slot, axis=0) * present[:, None, None].astype(
        jnp.bfloat16
    )
    incoming = lax.all_to_all(outgoing, "store", split_axis=0, concat_axis=0, tiled=True)
    my_owners = lax.dynamic_index_in_dim(owners, store_rank, 0, keepdims=False)
    fetched = jnp.take(incoming, my_owners, axis=0)
    offsets = jnp.arange(PASSAGES) * PASSAGE
    old_keys = rotate(fetched[..., :HEAD_DIM].astype(jnp.float32), offsets[:, None]).astype(
        jnp.bfloat16
    )
    old_keys = old_keys.reshape(SEQ, HEAD_DIM)
    old_values = fetched[..., HEAD_DIM:].reshape(SEQ, HEAD_DIM)
    row_ids = jnp.arange(row_count, dtype=jnp.int32)
    target = jnp.where(row_ids < live_count, positions, SEQ)
    all_keys = old_keys.at[target].set(new_keys, mode="drop")
    all_values = old_values.at[target].set(new_values, mode="drop")
    allowed = jnp.arange(SEQ, dtype=jnp.int32)[None, :] <= positions[:, None]
    scores = jnp.einsum("rgd,sd->grs", queries, all_keys, preferred_element_type=jnp.float32)
    scores = jnp.where(allowed[None], scores, -jnp.inf)
    row_max = jnp.max(scores, axis=-1, keepdims=True)
    shifted = jnp.exp(scores - row_max)
    weight = (shifted / jnp.sum(shifted, axis=-1, keepdims=True)).astype(jnp.bfloat16)
    context = jnp.einsum("grs,sd->rgd", weight, all_values, preferred_element_type=jnp.float32)
    row_live = (row_ids < live_count)[:, None, None]
    context = jnp.where(row_live, context, 0.0)
    return context.reshape(1, row_count, local_heads * HEAD_DIM).astype(jnp.bfloat16)


def solution(mesh):
    split = Mesh(mesh.devices.reshape(mesh.shape["store"], 2, 8), ("store", "tp_0", "tp_1"))
    placed = (
        P("store", None, TP),
        P(None, TP),
        P(TP, None),
        P("store", None, None, None),
        P(),
        P("store", None),
        P("store"),
    )
    return jax.shard_map(
        local, mesh=split, in_specs=placed, out_specs=P("store", None, TP), check_vma=False
    )
```

profile of v0, /device:TPU:33, one launch (start us, length us, event | category | flops | bytes accessed | tf_op | source)
XLA Modules:
  0.0 259.8 jit_solution(8467378492987644100)
XLA Ops:
  7.3 32.1 %all-gather.5.cloned.1.call-done = bf16[2,576,512]{2,1,0:T(8,128)(2,1)} async-done(((bf16[1,576,512]{2,1,0:T(8,128)(2,1)}), bf16[2,576,512]{2,1,0:T(8,128)(2,1)}) %all-gather.5.cloned.1.call-update) | async-done | bytes 1179664 | tf_op jit(solution)/shard_map/all_gather | solution.py:43
  39.5 3.2 %convolution_convert_fusion = bf16[576,1024]{1,0:T(8,128)(2,1)} fusion(bf16[512,1024]{1,0:T(8,128)(2,1)} %param.9, bf16[1,576,512]{2,1,0:T(8,128)(2,1)} %param.7), kind=kOutput, calls=%fused_computation.19 | convolution fusion | flops 604569600 | bytes 2818048 | tf_op jit(solution)/shard_map/dot_general | solution.py:77
  42.7 2.4 copy.39
  45.1 6.9 %all-to-all-start.1 = ((bf16[16,576,64]{1,2,0:T(8,128)(2,1)}), bf16[16,576,64]{1,2,0:T(8,128)(2,1)}, u32[]{:S(2)}, u32[]{:S(2)}) async-start(bf16[16,576,64]{1,2,0:T(8,128)(2,1)} %bitcast.72), calls=%async_computation.1 | async-start | bytes 2621440 | tf_op jit(solution)/shard_map/all_to_all | solution.py:26
  53.1 1.9 gather_fusion
  55.0 2.0 select_multiply_fusion
  57.0 33.9 %all-to-all-done.1 = bf16[16,576,64]{1,2,0:T(8,128)(2,1)} async-done(((bf16[16,576,64]{1,2,0:T(8,128)(2,1)}), bf16[16,576,64]{1,2,0:T(8,128)(2,1)}, u32[]{:S(2)}, u32[]{:S(2)}) %all-to-all-start.1) | async-done | bytes 1179680 | tf_op jit(solution)/shard_map/all_to_all | solution.py:26
  90.9 12.1 %all-to-all-start = ((bf16[16,384,256]{2,1,0:T(8,128)(2,1)}), bf16[16,384,256]{2,1,0:T(8,128)(2,1)S(1)}, u32[]{:S(2)}, u32[]{:S(2)}) async-start(bf16[16,384,256]{2,1,0:T(8,128)(2,1)} %select_multiply_fusion), calls=%async_computation | async-start | bytes 6291456 | tf_op jit(solution)/shard_map/all_to_all | solution.py:112
  104.0 2.6 iota_compare_fusion
  108.2 4.4 %collective-permute-start = (bf16[576,64]{0,1:T(8,128)(2,1)S(1)}, bf16[576,64]{0,1:T(8,128)(2,1)S(1)}, u32[]{:S(2)}, u32[]{:S(2)}) collective-permute-start(bf16[576,64]{0,1:T(8,128)(2,1)S(1)} %convert_element_type.92), channel_id=1, source_target_pairs={{0,1},{1,0},{2,3},{3,2},{4,5},{5,4},{6,7},{7,6},{8,9},{9,8},{10,11... | collective-permute-start | bytes 221192 | tf_op jit(solution)/shard_map/ppermute | solution.py:31
  112.5 4.9 %collective-permute-done = bf16[576,64]{0,1:T(8,128)(2,1)S(1)} collective-permute-done((bf16[576,64]{0,1:T(8,128)(2,1)S(1)}, bf16[576,64]{0,1:T(8,128)(2,1)S(1)}, u32[]{:S(2)}, u32[]{:S(2)}) %collective-permute-start) | collective-permute-done | bytes 73760 | tf_op jit(solution)/shard_map/ppermute | solution.py:31
  118.3 11.2 %collective-permute-done.1 = bf16[576,128]{0,1:T(8,128)(2,1)} collective-permute-done((bf16[576,128]{0,1:T(8,128)(2,1)}, bf16[576,128]{0,1:T(8,128)(2,1)}, u32[]{:S(2)}, u32[]{:S(2)}) %collective-permute-start.1) | collective-permute-done | bytes 147488 | tf_op jit(solution)/shard_map/ppermute | solution.py:31
  131.2 11.4 %all-to-all-done = bf16[16,384,256]{2,1,0:T(8,128)(2,1)S(1)} async-done(((bf16[16,384,256]{2,1,0:T(8,128)(2,1)}), bf16[16,384,256]{2,1,0:T(8,128)(2,1)S(1)}, u32[]{:S(2)}, u32[]{:S(2)}) %all-to-all-start) | async-done | bytes 3145760 | tf_op jit(solution)/shard_map/all_to_all | solution.py:112
  142.6 1.8 gather_fusion.1
  148.3 30.5 %all-gather.7.cloned.1.call-done = bf16[16,576,512]{2,1,0:T(8,128)(2,1)} async-done(((bf16[2,576,512]{2,1,0:T(8,128)(2,1)}), bf16[16,576,512]{2,1,0:T(8,128)(2,1)}) %all-gather.7.cloned.1.call-update) | async-done | bytes 9437200 | tf_op jit(solution)/shard_map/all_gather | solution.py:43
  178.7 8.2 %copy.40 = bf16[2,8,1,576,512]{4,3,1,0,2:T(8,128)(2,1)} copy(bf16[2,8,1,576,512]{4,3,0,1,2:T(8,128)(2,1)} %bitcast.70) | data formatting | bytes 18874368 | tf_op jit(solution)/shard_map/transpose | solution.py:47
  186.9 5.7 %multiply_reduce_fusion = f32[576]{0:T(1024)S(1)} fusion(bf16[1,576,16,512]{3,1,2,0:T(8,128)(2,1)} %bitcast.68), kind=kLoop, calls=%fused_computation.5 | loop fusion | flops 14155200 | bytes 9439488 | tf_op jit(solution)/shard_map/reduce_sum | solution.py:91
  195.7 8.7 %copy.53 = bf16[72,8,16,512]{3,1,2,0:T(8,128)(2,1)} copy(bf16[72,8,16,512]{3,1,0,2:T(8,128)(2,1)} %bitcast.69) | data formatting | bytes 18874368
  204.4 10.7 %convolution_multiply_fusion = f32[576,256]{0,1:T(8,128)S(1)} fusion(bf16[576,8192]{1,0:T(8,128)(2,1)} %bitcast.71, bf16[8192,256]{1,0:T(8,128)(2,1)} %param.8, f32[576]{0:T(1024)S(1)} %add_rsqrt_fusion), kind=kOutput, calls=%fused_computation.21 | convolution fusion | flops 2416066560 | bytes 14223616 | tf_op jit(solution)/shard_map/dot_general | solution.py:90
  218.9 1.7 copy.41
  220.6 5.0 %scatter_fusion.1 = bf16[3072,128]{1,0:T(8,128)(2,1)S(1)} fusion(bf16[3072,128]{1,0:T(8,128)(2,1)S(1)} %pad_maximum_fusion, s32[576]{0:T(1024)S(1)} %fusion.25, bf16[576,128]{1,0:T(8,128)(2,1)} %copy.42), kind=kCustom, calls=%fused_computation.3 | custom fusion | bytes 444672 | tf_op jit(solution)/shard_map/scatter | solution.py:123
  225.6 5.3 %scatter_fusion = bf16[3072,128]{1,0:T(8,128)(2,1)S(1)} fusion(bf16[3072,128]{1,0:T(8,128)(2,1)S(1)} %bitcast.73, s32[576]{0:T(1024)S(1)} %fusion.25, bf16[576,128]{1,0:T(8,128)(2,1)} %copy.41), kind=kCustom, calls=%fused_computation.2 | custom fusion | bytes 444672 | tf_op jit(solution)/shard_map/scatter | solution.py:124
  232.2 12.1 %fusion.33 = (f32[2,576]{1,0:T(2,128)S(1)}, f32[2,576,3072]{2,1,0:T(8,128)}) fusion(pred[576,3072]{1,0:T(8,128)(4,1)} %iota_compare_fusion, bf16[3072,128]{1,0:T(8,128)(2,1)S(1)} %scatter_fusion.1, f32[576,2,64]{2,0,1:T(8,128)} %get-tuple-element.11, f32[576,2,64]{2,0,1:T(8,128)} %get-tuple-element.10), kind=kOutput, calls=%fused_computation.82 | convolution fusion | flops 917031936 | bytes 17306112 | tf_op jit(solution)/shard_map/sub | solution.py:129
  244.2 7.5 %fusion.9 = bf16[576,2,128]{2,0,1:T(8,128)(2,1)S(1)} fusion(f32[2,576,3072]{2,1,0:T(8,128)} %get-tuple-element.25, f32[2,576]{1,0:T(2,128)S(1)} %get-tuple-element.24, bf16[3072,128]{1,0:T(8,128)(2,1)} %copy-done.3, pred[576]{0:T(1024)(128)(4,1)S(1)} %iota_compare_fusion.1), kind=kOutput, calls=%fused_computation.24 | convolution fusion | flops 913342464 | bytes 15242304 | tf_op jit(solution)/shard_map/grs,sd->rgd/dot_general | solution.py:131
  (62 shorter events, 19.3 us)
Async XLA Ops:
  6.5 45.6 %copy-start = (bf16[4,4,384,256]{3,2,1,0:T(8,128)(2,1)S(1)}, bf16[4,4,384,256]{3,2,1,0:T(8,128)(2,1)}, u32[]{:S(2)}) copy-start(bf16[4,4,384,256]{3,2,1,0:T(8,128)(2,1)} %param.10) | copy-start | bytes 9437188
  6.5 32.9 %all-gather.5.cloned.1.call-start = ((), (), s32[]{:S(2)}) async-start(), calls=%async_computation.2 | async-start | bytes 1769472 | tf_op jit(solution)/shard_map/all_gather | solution.py:43
  7.3 171.5 %all-gather.7.cloned.1.call-start = ((), (), s32[]{:S(2)}) async-start(), calls=%async_computation.3 | async-start | bytes 10616832 | tf_op jit(solution)/shard_map/all_gather | solution.py:43
  42.7 9.4 %copy-start.6 = (s32[16,8]{0,1:T(8,128)S(1)}, s32[16,8]{0,1:T(8,128)}, u32[]{:S(2)}) copy-start(s32[16,8]{0,1:T(8,128)} %param.11) | copy-start | bytes 1540
  45.1 45.8 %all-to-all-start.1 = ((bf16[16,576,64]{1,2,0:T(8,128)(2,1)}), bf16[16,576,64]{1,2,0:T(8,128)(2,1)}, u32[]{:S(2)}, u32[]{:S(2)}) async-start(bf16[16,576,64]{1,2,0:T(8,128)(2,1)} %bitcast.72), calls=%async_computation.1 | async-start | bytes 2621440 | tf_op jit(solution)/shard_map/all_to_all | solution.py:26
  57.0 46.0 %copy-start.7 = (s32[1,576]{1,0:T(1,128)S(1)}, s32[1,576]{1,0:T(1,128)}, u32[]{:S(2)}) copy-start(s32[1,576]{1,0:T(1,128)} %param.12) | copy-start | bytes 6916
  90.9 51.7 %all-to-all-start = ((bf16[16,384,256]{2,1,0:T(8,128)(2,1)}), bf16[16,384,256]{2,1,0:T(8,128)(2,1)S(1)}, u32[]{:S(2)}, u32[]{:S(2)}) async-start(bf16[16,384,256]{2,1,0:T(8,128)(2,1)} %select_multiply_fusion), calls=%async_computation | async-start | bytes 6291456 | tf_op jit(solution)/shard_map/all_to_all | solution.py:112
  108.2 9.3 %collective-permute-start = (bf16[576,64]{0,1:T(8,128)(2,1)S(1)}, bf16[576,64]{0,1:T(8,128)(2,1)S(1)}, u32[]{:S(2)}, u32[]{:S(2)}) collective-permute-start(bf16[576,64]{0,1:T(8,128)(2,1)S(1)} %convert_element_type.92), channel_id=1, source_target_pairs={{0,1},{1,0},{2,3},{3,2},{4,5},{5,4},{6,7},{7,6},{8,9},{9,8},{10,11... | collective-permute-start | bytes 221192 | tf_op jit(solution)/shard_map/ppermute | solution.py:31
  118.2 11.3 %collective-permute-start.1 = (bf16[576,128]{0,1:T(8,128)(2,1)}, bf16[576,128]{0,1:T(8,128)(2,1)}, u32[]{:S(2)}, u32[]{:S(2)}) collective-permute-start(bf16[576,128]{0,1:T(8,128)(2,1)} %get-tuple-element.5), channel_id=1, source_target_pairs={{0,2},{1,3},{2,0},{3,1},{4,6},{5,7},{6,4},{7,5},{8,10},{9,11},{10,... | collective-permute-start | bytes 442376 | tf_op jit(solution)/shard_map/ppermute | solution.py:31
  186.9 5.7 %copy-start.4 = (f32[576,128]{0,1:T(8,128)S(1)}, f32[576,128]{0,1:T(8,128)}, u32[]{:S(2)}) copy-start(f32[576,128]{0,1:T(8,128)} %convert_element_type.95) | copy-start | bytes 884740
  215.1 10.5 %copy-start.2 = (bf16[8,384,128]{2,1,0:T(8,128)(2,1)S(1)}, bf16[8,384,128]{2,1,0:T(8,128)(2,1)}, u32[]{:S(2)}) copy-start(bf16[8,384,128]{2,1,0:T(8,128)(2,1)} %get-tuple-element.14) | copy-start | bytes 2359300
  215.6 15.3 %copy-start.5 = (f32[576,64]{1,0:T(8,128)S(1)}, f32[576,64]{1,0:T(8,128)}, u32[]{:S(2)}) copy-start(f32[576,64]{1,0:T(8,128)} %copy.48) | copy-start | bytes 442372
  230.9 13.3 %copy-start.3 = (bf16[3072,128]{1,0:T(8,128)(2,1)}, bf16[3072,128]{1,0:T(8,128)(2,1)S(1)}, u32[]{:S(2)}) copy-start(bf16[3072,128]{1,0:T(8,128)(2,1)S(1)} %scatter_fusion) | copy-start | bytes 2359300
  244.2 8.7 %copy-start.1 = (bf16[4,4,384,256]{3,2,1,0:T(8,128)(2,1)S(1)}, bf16[4,4,384,256]{3,2,1,0:T(8,128)(2,1)}, u32[]{:S(2)}) copy-start(bf16[4,4,384,256]{3,2,1,0:T(8,128)(2,1)} %param.10) | copy-start | bytes 9437188
Sparse Core Ops, SparseCore 0:
  9.1 30.2 all-gather.4
  41.2 137.4 all-gather.6
where the time goes:
time: 260 us
  waiting for transfers between devices  125 us (48%)
  local copies, waits for them, and re-layouts  41.2 us (16%)
  matrix products  33.4 us (13%)
  starting transfers between devices  23.5 us (9%)
  other arithmetic  22.5 us (9%)
  between operations  14.3 us (6%)
    all_gather x2, waiting for transfers between devices, stacked_from(): parts = lax.all_gather(parts, axes[k], axis=0, tiled=True)  62.6 us
    all_to_all x1, waiting for transfers between devices, summed_on_arrival(): lax.all_to_all(parts, axis, split_axis=0, concat_axis=0, tiled=True)  33.9 us
    ppermute x2, waiting for transfers between devices, from_partner(): lax.ppermute(value, axis, [(i, i ^ 1 << bit) for i in range(lax.axis_size...  16.2 us
    all_to_all x1, starting transfers between devices, local(): lax.all_to_all(outgoing, 'store', split_axis=0, concat_axis=0, tiled=True)  12.1 us
    sub x1, matrix products, local(): shifted = jnp.exp(scores - row_max)  12.1 us
    all_to_all x1, waiting for transfers between devices, local(): lax.all_to_all(outgoing, 'store', split_axis=0, concat_axis=0, tiled=True)  11.4 us
    dot_general x1, matrix products, local(): running = jnp.dot(token_part, w_query, preferred_element_type=jnp.float32)  10.7 us
    unnamed x19, local copies, waits for them, and re-layouts  9.17 us
  transfers between devices with their start and end apart: 6, of which 6 were waited for; matrix products, arithmetic and copies ran while one was open for 9% of the time, Pallas kernels for 0%

commit v1 on v0

--- a/solution.py
+++ b/solution.py
@@ -40,7 +40,9 @@
 def stacked_from(value, axes, sequence):
     parts = value[None]
     for k in sequence:
-        parts = lax.all_gather(parts, axes[k], axis=0, tiled=True)
+        parts = jnp.concatenate(
+            lax.all_to_all(jnp.stack([parts] * lax.axis_size(axes[k])), axes[k], 0, 0), axis=0
+        )
     held = [lax.axis_size(axes[k]) for k in reversed(sequence)]
     parts = parts.reshape(*held, *value.shape)
     turned = sorted(range(len(sequence)), key=lambda place: sequence[len(sequence) - 1 - place])

time: 260 us -> 419 us (1.61)
  waiting for transfers between devices: 125 us -> 237 us
  blocking collectives: 0 us -> 50 us
  between operations: 14.3 us -> 1.05 us
  local copies, waits for them, and re-layouts: 41.2 us -> 48.7 us
    ppermute x2, waiting for transfers between devices: 16.2 us -> 205 us  [from_partner(): lax.ppermute(value, axis, [(i, i ^ 1 << bit) for i in range(lax.axis_size...]
    all_gather x2 -> x0, waiting for transfers between devices: 62.6 us -> none  [stacked_from(): parts = lax.all_gather(parts, axes[k], axis=0, tiled=True)]
    all_to_all x0 -> x1, blocking collectives: none -> 50 us  [local(): lax.all_to_all(outgoing, 'store', split_axis=0, concat_axis=0, tiled=True)]
    all_to_all x1, waiting for transfers between devices: 33.9 us -> 22.6 us  [summed_on_arrival(): lax.all_to_all(parts, axis, split_axis=0, concat_axis=0, tiled=True)]
    all_to_all x0 -> x1, local copies, waits for them, and re-layouts: none -> 8.17 us  [stacked_from(): lax.all_to_all(jnp.stack([parts] * lax.axis_size(axes[k])), axes[k], 0, 0)]
    transpose x1 -> x0, local copies, waits for them, and re-layouts: 8.17 us -> none  [stacked_from(): parts.transpose(*turned, *range(len(sequence), parts.ndim))]
    another operation x0 -> x1, local copies, waits for them, and re-layouts: none -> 5.84 us  [stacked_from(): jnp.stack([parts] * lax.axis_size(axes[k]))]
    all_to_all x1 -> x2, waiting for transfers between devices: 11.4 us -> 8.86 us  [stacked_from(): lax.all_to_all(jnp.stack([parts] * lax.axis_size(axes[k])), axes[k], 0, 0)]
  transfers between devices with their start and end apart: 6 -> 5, of which waited for: 6 -> 4; matrix products, arithmetic and copies ran while one was open for 9% -> 6% of each run, Pallas kernels for 0% -> 0%
where the time goes in v1:
time: 419 us; the launch traced here: 417 us
  waiting for transfers between devices  237 us (57%)
  blocking collectives  50 us (12%)
  local copies, waits for them, and re-layouts  48.7 us (12%)
  matrix products  33.4 us (8%)
  other arithmetic  25.4 us (6%)
  starting transfers between devices  21 us (5%)
    ppermute x2, waiting for transfers between devices, from_partner(): lax.ppermute(value, axis, [(i, i ^ 1 << bit) for i in range(lax.axis_size...  205 us
    all_to_all x1, blocking collectives, local(): lax.all_to_all(outgoing, 'store', split_axis=0, concat_axis=0, tiled=True)  50 us
    all_to_all x1, waiting for transfers between devices, summed_on_arrival(): lax.all_to_all(parts, axis, split_axis=0, concat_axis=0, tiled=True)  22.6 us
    sub x1, matrix products, local(): shifted = jnp.exp(scores - row_max)  12.1 us
    dot_general x1, matrix products, local(): running = jnp.dot(token_part, w_query, preferred_element_type=jnp.float32)  10.7 us
    all_to_all x2, starting transfers between devices, stacked_from(): lax.all_to_all(jnp.stack([parts] * lax.axis_size(axes[k])), axes[k], 0, 0)  9.92 us
    unnamed x21, local copies, waits for them, and re-layouts  9.17 us
    all_to_all x2, waiting for transfers between devices, stacked_from(): lax.all_to_all(jnp.stack([parts] * lax.axis_size(axes[k])), axes[k], 0, 0)  8.86 us
  transfers between devices with their start and end apart: 5, of which 4 were waited for; matrix products, arithmetic and copies ran while one was open for 6% of the time, Pallas kernels for 0%

profile of v1, /device:TPU:33, one launch (start us, length us, event | category | flops | bytes accessed | tf_op | source)
XLA Modules:
  0.0 416.5 jit_solution(3603044836555482971)
XLA Ops:
  0.0 2.5 pad_maximum_fusion
  2.5 4.5 %all-to-all-start.2 = ((bf16[2,1,1,576,512]{4,3,2,1,0:T(8,128)(2,1)}), bf16[2,1,1,576,512]{4,3,2,1,0:T(8,128)(2,1)}, u32[]{:S(2)}, u32[]{:S(2)}) async-start(bf16[2,1,1,576,512]{4,3,2,1,0:T(8,128)(2,1)} %pad_maximum_fusion), calls=%async_computation.2 | async-start | bytes 2359296 | tf_op jit(solution)/shard_map/all_to_all | solution.py:44
  7.0 3.2 convolution_convert_fusion
  10.2 2.4 copy.33
  12.7 8.9 %all-to-all-done.2 = bf16[2,1,1,576,512]{4,3,2,1,0:T(8,128)(2,1)} async-done(((bf16[2,1,1,576,512]{4,3,2,1,0:T(8,128)(2,1)}), bf16[2,1,1,576,512]{4,3,2,1,0:T(8,128)(2,1)}, u32[]{:S(2)}, u32[]{:S(2)}) %all-to-all-start.2) | async-done | bytes 1179680 | tf_op jit(solution)/shard_map/all_to_all | solution.py:44
  21.5 8.0 %all-to-all-start.1 = ((bf16[16,576,64]{1,2,0:T(8,128)(2,1)}), bf16[16,576,64]{1,2,0:T(8,128)(2,1)}, u32[]{:S(2)}, u32[]{:S(2)}) async-start(bf16[16,576,64]{1,2,0:T(8,128)(2,1)} %bitcast.72), calls=%async_computation.1 | async-start | bytes 2621440 | tf_op jit(solution)/shard_map/all_to_all | solution.py:26
  30.6 3.5 gather_fusion
  34.2 2.3 select_multiply_fusion
  36.4 22.6 %all-to-all-done.1 = bf16[16,576,64]{1,2,0:T(8,128)(2,1)} async-done(((bf16[16,576,64]{1,2,0:T(8,128)(2,1)}), bf16[16,576,64]{1,2,0:T(8,128)(2,1)}, u32[]{:S(2)}, u32[]{:S(2)}) %all-to-all-start.1) | async-done | bytes 1179680 | tf_op jit(solution)/shard_map/all_to_all | solution.py:26
  59.0 50.0 %all_to_all.20 = bf16[16,384,256]{2,1,0:T(8,128)(2,1)} all-to-all(bf16[16,384,256]{2,1,0:T(8,128)(2,1)S(1)} %select_multiply_fusion), channel_id=1, replica_groups=mesh['store'=16,'tp_0'=2,'tp_1'=8] {'store'}, dimensions={0} | all-to-all | bytes 6291456 | tf_op jit(solution)/shard_map/all_to_all | solution.py:114
  109.0 5.8 %stack.7 = bf16[8,2,1,576,512]{4,3,1,2,0:T(8,128)(2,1)} broadcast(bf16[2,576,512]{2,1,0:T(8,128)(2,1)} %bitcast.11), dimensions={1,3,4} | broadcast | bytes 10616832 | tf_op jit(solution)/shard_map/stack | solution.py:44
  114.8 5.4 %all-to-all-start.3 = ((bf16[8,2,1,576,512]{4,3,1,2,0:T(8,128)(2,1)}), bf16[8,2,1,576,512]{4,3,1,2,0:T(8,128)(2,1)}, u32[]{:S(2)}, u32[]{:S(2)}) async-start(bf16[8,2,1,576,512]{4,3,1,2,0:T(8,128)(2,1)} %stack.7), calls=%async_computation.3 | async-start | bytes 18874368 | tf_op jit(solution)/shard_map/all_to_all | solution.py:44
  121.4 2.6 iota_compare_fusion
  125.9 199.5 %collective-permute-done = bf16[576,64]{0,1:T(8,128)(2,1)S(1)} collective-permute-done((bf16[576,64]{0,1:T(8,128)(2,1)S(1)}, bf16[576,64]{0,1:T(8,128)(2,1)S(1)}, u32[]{:S(2)}, u32[]{:S(2)}) %collective-permute-start) | collective-permute-done | bytes 73760 | tf_op jit(solution)/shard_map/ppermute | solution.py:31
  326.0 2.8 collective-permute-start.1
  328.9 6.0 %collective-permute-done.1 = bf16[576,128]{0,1:T(8,128)(2,1)} collective-permute-done((bf16[576,128]{0,1:T(8,128)(2,1)}, bf16[576,128]{0,1:T(8,128)(2,1)}, u32[]{:S(2)}, u32[]{:S(2)}) %collective-permute-start.1) | collective-permute-done | bytes 147488 | tf_op jit(solution)/shard_map/ppermute | solution.py:31
  342.3 8.2 %copy.34 = bf16[8,2,1,576,512]{4,3,0,1,2:T(8,128)(2,1)} copy(bf16[8,2,1,576,512]{4,3,1,2,0:T(8,128)(2,1)} %all-to-all-done.3) | data formatting | bytes 18874368 | tf_op jit(solution)/shard_map/all_to_all | solution.py:44
  350.5 5.7 %multiply_reduce_fusion = f32[576]{0:T(1024)S(1)} fusion(bf16[1,576,16,512]{3,1,2,0:T(8,128)(2,1)} %bitcast.69), kind=kLoop, calls=%fused_computation.5 | loop fusion | flops 14155200 | bytes 9439488 | tf_op jit(solution)/shard_map/reduce_sum | solution.py:93
  359.2 8.7 %copy.47 = bf16[72,8,16,512]{3,1,2,0:T(8,128)(2,1)} copy(bf16[72,8,16,512]{3,1,0,2:T(8,128)(2,1)} %bitcast.70) | data formatting | bytes 18874368
  367.9 10.7 %convolution_multiply_fusion = f32[576,256]{0,1:T(8,128)S(1)} fusion(bf16[576,8192]{1,0:T(8,128)(2,1)} %bitcast.71, bf16[8192,256]{1,0:T(8,128)(2,1)} %param.8, f32[576]{0:T(1024)S(1)} %add_rsqrt_fusion), kind=kOutput, calls=%fused_computation.21 | convolution fusion | flops 2416066560 | bytes 14223616 | tf_op jit(solution)/shard_map/dot_general | solution.py:92
  384.1 5.0 %scatter_fusion.1 = bf16[3072,128]{1,0:T(8,128)(2,1)S(1)} fusion(bf16[3072,128]{1,0:T(8,128)(2,1)S(1)} %pad_maximum_fusion.1, s32[576]{0:T(1024)S(1)} %fusion.25, bf16[576,128]{1,0:T(8,128)(2,1)} %copy.36), kind=kCustom, calls=%fused_computation.3 | custom fusion | bytes 444672 | tf_op jit(solution)/shard_map/scatter | solution.py:125
  389.2 5.3 %scatter_fusion = bf16[3072,128]{1,0:T(8,128)(2,1)S(1)} fusion(bf16[3072,128]{1,0:T(8,128)(2,1)S(1)} %bitcast.73, s32[576]{0:T(1024)S(1)} %fusion.25, bf16[576,128]{1,0:T(8,128)(2,1)} %copy.35), kind=kCustom, calls=%fused_computation.2 | custom fusion | bytes 444672 | tf_op jit(solution)/shard_map/scatter | solution.py:126
  395.7 12.1 %fusion.33 = (f32[2,576]{1,0:T(2,128)S(1)}, f32[2,576,3072]{2,1,0:T(8,128)}) fusion(pred[576,3072]{1,0:T(8,128)(4,1)} %iota_compare_fusion, bf16[3072,128]{1,0:T(8,128)(2,1)S(1)} %scatter_fusion.1, f32[576,2,64]{2,0,1:T(8,128)} %get-tuple-element.11, f32[576,2,64]{2,0,1:T(8,128)} %get-tuple-element.10), kind=kOutput, calls=%fused_computation.83 | convolution fusion | flops 917031936 | bytes 17306112 | tf_op jit(solution)/shard_map/sub | solution.py:131
  407.8 7.5 %fusion.9 = bf16[576,2,128]{2,0,1:T(8,128)(2,1)S(1)} fusion(f32[2,576,3072]{2,1,0:T(8,128)} %get-tuple-element.25, f32[2,576]{1,0:T(2,128)S(1)} %get-tuple-element.24, bf16[3072,128]{1,0:T(8,128)(2,1)} %copy-done.4, pred[576]{0:T(1024)(128)(4,1)S(1)} %iota_compare_fusion.1), kind=kOutput, calls=%fused_computation.25 | convolution fusion | flops 913342464 | bytes 15242304 | tf_op jit(solution)/shard_map/grs,sd->rgd/dot_general | solution.py:133
  (63 shorter events, 22.3 us)
Async XLA Ops:
  0.0 29.6 %copy-start = (bf16[4,4,384,256]{3,2,1,0:T(8,128)(2,1)S(1)}, bf16[4,4,384,256]{3,2,1,0:T(8,128)(2,1)}, u32[]{:S(2)}) copy-start(bf16[4,4,384,256]{3,2,1,0:T(8,128)(2,1)} %param.10) | copy-start | bytes 9437188
  2.5 19.0 %all-to-all-start.2 = ((bf16[2,1,1,576,512]{4,3,2,1,0:T(8,128)(2,1)}), bf16[2,1,1,576,512]{4,3,2,1,0:T(8,128)(2,1)}, u32[]{:S(2)}, u32[]{:S(2)}) async-start(bf16[2,1,1,576,512]{4,3,2,1,0:T(8,128)(2,1)} %pad_maximum_fusion), calls=%async_computation.2 | async-start | bytes 2359296 | tf_op jit(solution)/shard_map/all_to_all | solution.py:44
  10.2 19.3 %copy-start.7 = (s32[16,8]{0,1:T(8,128)S(1)}, s32[16,8]{0,1:T(8,128)}, u32[]{:S(2)}) copy-start(s32[16,8]{0,1:T(8,128)} %param.11) | copy-start | bytes 1540
  21.5 37.5 %all-to-all-start.1 = ((bf16[16,576,64]{1,2,0:T(8,128)(2,1)}), bf16[16,576,64]{1,2,0:T(8,128)(2,1)}, u32[]{:S(2)}, u32[]{:S(2)}) async-start(bf16[16,576,64]{1,2,0:T(8,128)(2,1)} %bitcast.72), calls=%async_computation.1 | async-start | bytes 2621440 | tf_op jit(solution)/shard_map/all_to_all | solution.py:26
  114.8 5.4 %copy-start.8 = (s32[1,576]{1,0:T(1,128)S(1)}, s32[1,576]{1,0:T(1,128)}, u32[]{:S(2)}) copy-start(s32[1,576]{1,0:T(1,128)} %param.12) | copy-start | bytes 6916
  114.8 227.5 %all-to-all-start.3 = ((bf16[8,2,1,576,512]{4,3,1,2,0:T(8,128)(2,1)}), bf16[8,2,1,576,512]{4,3,1,2,0:T(8,128)(2,1)}, u32[]{:S(2)}, u32[]{:S(2)}) async-start(bf16[8,2,1,576,512]{4,3,1,2,0:T(8,128)(2,1)} %stack.7), calls=%async_computation.3 | async-start | bytes 18874368 | tf_op jit(solution)/shard_map/all_to_all | solution.py:44
  120.3 216.3 %copy-start.2 = (bf16[16,384,256]{2,1,0:T(8,128)(2,1)S(1)}, bf16[16,384,256]{2,1,0:T(8,128)(2,1)}, u32[]{:S(2)}) copy-start(bf16[16,384,256]{2,1,0:T(8,128)(2,1)} %all_to_all.20) | copy-start | bytes 9437188
  125.6 199.7 %collective-permute-start = (bf16[576,64]{0,1:T(8,128)(2,1)S(1)}, bf16[576,64]{0,1:T(8,128)(2,1)S(1)}, u32[]{:S(2)}, u32[]{:S(2)}) collective-permute-start(bf16[576,64]{0,1:T(8,128)(2,1)S(1)} %convert_element_type.92), channel_id=1, source_target_pairs={{0,1},{1,0},{2,3},{3,2},{4,5},{5,4},{6,7},{7,6},{8,9},{9,8},{10,11... | collective-permute-start | bytes 221192 | tf_op jit(solution)/shard_map/ppermute | solution.py:31
  326.0 8.9 %collective-permute-start.1 = (bf16[576,128]{0,1:T(8,128)(2,1)}, bf16[576,128]{0,1:T(8,128)(2,1)}, u32[]{:S(2)}, u32[]{:S(2)}) collective-permute-start(bf16[576,128]{0,1:T(8,128)(2,1)} %get-tuple-element.5), channel_id=1, source_target_pairs={{0,2},{1,3},{2,0},{3,1},{4,6},{5,7},{6,4},{7,5},{8,10},{9,11},{10,... | collective-permute-start | bytes 442376 | tf_op jit(solution)/shard_map/ppermute | solution.py:31
  350.5 5.7 %copy-start.5 = (f32[576,128]{0,1:T(8,128)S(1)}, f32[576,128]{0,1:T(8,128)}, u32[]{:S(2)}) copy-start(f32[576,128]{0,1:T(8,128)} %convert_element_type.95) | copy-start | bytes 884740
  378.6 10.6 %copy-start.3 = (bf16[8,384,128]{2,1,0:T(8,128)(2,1)S(1)}, bf16[8,384,128]{2,1,0:T(8,128)(2,1)}, u32[]{:S(2)}) copy-start(bf16[8,384,128]{2,1,0:T(8,128)(2,1)} %get-tuple-element.14) | copy-start | bytes 2359300
  379.1 15.4 %copy-start.6 = (f32[576,64]{1,0:T(8,128)S(1)}, f32[576,64]{1,0:T(8,128)}, u32[]{:S(2)}) copy-start(f32[576,64]{1,0:T(8,128)} %copy.42) | copy-start | bytes 442372
  394.5 13.3 %copy-start.4 = (bf16[3072,128]{1,0:T(8,128)(2,1)}, bf16[3072,128]{1,0:T(8,128)(2,1)S(1)}, u32[]{:S(2)}) copy-start(bf16[3072,128]{1,0:T(8,128)(2,1)S(1)} %scatter_fusion) | copy-start | bytes 2359300
  407.8 8.7 %copy-start.1 = (bf16[4,4,384,256]{3,2,1,0:T(8,128)(2,1)S(1)}, bf16[4,4,384,256]{3,2,1,0:T(8,128)(2,1)}, u32[]{:S(2)}) copy-start(bf16[4,4,384,256]{3,2,1,0:T(8,128)(2,1)} %param.10) | copy-start | bytes 9437188
